TPU v7x, 256 devices: a whole 4x4x8 slice. The times are simulated.
256 devices in a mesh: node: 8 (over x, core), space: 32 (over y, z).
Axes of the slice: x: 4, y: 4, z: 8, core: 2. Of those that a mesh axis runs over, the one named last changes fastest.
Arguments:
- initial: float32 [128, 256, 256], P('space'), may hold values from -1 to 1
- kappa: float32 [128, 256, 256], P('space'), may hold values from 0.3 to 3
Outputs:
- sections: float32 [8, 128, 256, 256], P('node', 'space')
All inputs are finite; a program needn't handle non-finite values.
Results may differ from a plain program's by a relative error of at most 0.0002.
Values sent between devices are 32-bit elements; how exact they have to be, the bound alone decides.
A program may use at most 192 MiB of HBM per device.

v0:
```python
import functools

import jax
import jax.numpy as jnp
import numpy as np
from jax import lax
from jax.experimental import pallas as pl
from jax.experimental.pallas import tpu as pltpu
from jax.sharding import PartitionSpec as P

SWEEPS = 2
VCYCLES = 2
COARSE = 8
DIFFUSE = 2.0
REACT = 0.5
OMEGA = 0.8
MESH = pl.DeviceIdType.MESH
HIGH = lax.Precision.HIGHEST

NY = 4
NZ = 8
NX = 4
DIRS = [(a, b) for a in (-1, 0, 1) for b in (-1, 0, 1) if (a, b) != (0, 0)]


def radau_gap(count, where):
    previous = 1.0
    current = where
    for degree in range(1, count):
        following = ((2 * degree + 1) * where * current - degree * previous) / (degree + 1)
        previous = current
        current = following
    return current - previous


def radau_table(count):
    zeros_found = []
    grid_count = 4096
    lower = -1.0
    value_low = radau_gap(count, lower)
    for place in range(1, grid_count):
        upper = -1.0 + 2.0 * place / grid_count
        value_up = radau_gap(count, upper)
        if value_low * value_up < 0.0:
            left_end = lower
            right_end = upper
            left_value = value_low
            for halving in range(100):
                middle = 0.5 * (left_end + right_end)
                middle_value = radau_gap(count, middle)
                if left_value * middle_value <= 0.0:
                    right_end = middle
                else:
                    left_end = middle
                    left_value = middle_value
            zeros_found.append(0.5 * (left_end + right_end))
        lower = upper
        value_low = value_up
    zeros_found.append(1.0)
    abscissa = [(value + 1.0) / 2.0 for value in zeros_found]
    table_rows = []
    for outer in range(count):
        table_rows.append([0.0] * count)
    for column in range(count):
        factor = [1.0]
        scale = 1.0
        for other in range(count):
            if other != column:
                widened = [0.0] * (len(factor) + 1)
                for power in range(len(factor)):
                    widened[power + 1] = widened[power + 1] + factor[power]
                    widened[power] = widened[power] - abscissa[other] * factor[power]
                factor = widened
                scale = scale * (abscissa[column] - abscissa[other])
        for outer in range(count):
            upto = abscissa[outer]
            accum = 0.0
            for power in range(len(factor)):
                accum = accum + factor[power] * upto ** (power + 1) / (power + 1)
            table_rows[outer][column] = accum / scale
    return (abscissa, table_rows)


def coefficients(count):
    abscissa, table_rows = radau_table(count)
    rows = []
    for m in range(count):
        shift = DIFFUSE * abscissa[m]
        row = list(table_rows[m]) + [shift, sum(table_rows[m])]
        for level in range(3):
            s = shift / 4.0**level
            a = OMEGA / (1.0 + 6.0 * s)
            row += [a, a * s, 1.0 + 6.0 * s, s]
        rows.append(row + [0.0] * (24 - len(row)))
    return np.asarray(rows, np.float32)


def sides(c):
    r, l = c.shape
    total = pltpu.roll(c, 1, 0) + pltpu.roll(c, r - 1, 0)
    return total + (pltpu.roll(c, 1, 1) + pltpu.roll(c, l - 1, 1))


def sweep_planes(src, first, count, parts, use):
    each = count // parts

    def part(i, _):
        start = first + i * each
        before = src[start - 1]
        here = src[start]
        for k in range(each):
            p = start + k
            after = src[p + 1]
            use(p, here, before + after + sides(here))
            before, here = here, after
        return 0

    if parts == 1:
        part(0, 0)
    else:
        lax.fori_loop(0, parts, part, 0)


def smooth(src, dst, f, a, b, first, count, parts):
    def use(p, here, total):
        dst[p] = (1.0 - OMEGA) * here + (a * f[p] + b * total)

    sweep_planes(src, first, count, parts, use)


def kernel(
    co, initial, kappa, pick0, pick1, back0, back1, out,
    uk, a0, b0, f0, la, kx, fg, rs, st, w0, xw,
    a1, b1, f1, rs1, st1, w1, f2, va, vb,
    in_s, in_r, xi, xq, halo_s, halo_r, out_s, out_r,
):
    node = lax.axis_index("node")
    space = lax.axis_index("space")
    x, core = node // 2, lax.rem(node, 2)
    y, z = space // NZ, lax.rem(space, NZ)
    n, m = NZ * 4, a0.shape[1] - 8

    def at(dx=0, dc=0, dy=0, dz=0):
        nx = lax.rem(x + dx + NX, NX)
        nc = lax.rem(core + dc, 2)
        ny = lax.rem(y + dy + NY, NY)
        nz = lax.rem(z + dz + NZ, NZ)
        return (nx * 2 + nc, ny * NZ + nz)

    peers = [at(dz=d) for d in range(1, NZ)]
    peers += [at(dy=a, dz=b) for a in (-1, 1) for b in (-1, 0, 1)]
    peers += [at(dx=1), at(dx=-1), at(dc=1)]
    barrier = pltpu.get_barrier_semaphore()
    for peer in peers:
        pl.semaphore_signal(barrier, inc=1, device_id=peer, device_id_type=MESH)
    pl.semaphore_wait(barrier, len(peers))

    def remote(src, dst, send, recv, device):
        return pltpu.make_async_remote_copy(
            src_ref=src, dst_ref=dst, send_sem=send, recv_sem=recv, device_id=device, device_id_type=MESH
        )

    def exchange(kind, src, dst, origin, planes, rows, width):
        total = src.shape[1]

        def span(step, size, start, wrap):
            if step == 0:
                return pl.ds(start, size), pl.ds(start, size)
            if step < 0:
                return pl.ds(start, width), pl.ds(start + size, width)
            return pl.ds(start + size - width, width), pl.ds(wrap, width)

        copies = []
        for d, (a, b) in enumerate(DIRS):
            ps, pd = span(a, planes, origin, origin - width)
            qs, qd = span(b, rows, 0, total - width)
            copies.append(
                remote(src.at[ps, qs], dst.at[pd, qd], halo_s.at[kind, d], halo_r.at[kind, d], at(dy=a, dz=b))
            )
        for copy in copies:
            copy.start()
        return copies

    def finish(copies):
        for copy in copies:
            copy.wait_recv()
        for copy in copies:
            copy.wait_send()

    def xgather(sem, piece, both, order, ready, done):
        own = {}
        for q in order:
            ready(q)
            own[q] = [
                remote(piece(x, q), piece(x, q), sem.at[0, q], sem.at[1, q], at(dx=1)),
                remote(piece(x, q), piece(x, q), sem.at[2, q], sem.at[3, q], at(dx=-1)),
            ]
            for copy in own[q]:
                copy.start()
        left, right = lax.rem(x + NX - 1, NX), lax.rem(x + 1, NX)
        passed, cores = {}, {}
        for q in order:
            own[q][0].wait_recv()
            if q % 2 == 0:
                passed[q] = remote(piece(left, q), piece(left, q), sem.at[4, q], sem.at[5, q], at(dx=1))
                passed[q].start()
            own[q][1].wait_recv()
            if q % 2 == 1:
                passed[q] = remote(piece(right, q), piece(right, q), sem.at[4, q], sem.at[5, q], at(dx=-1))
                passed[q].start()
        for q in order:
            passed[q].wait_recv()
            cores[q] = remote(both(q), both(q), sem.at[6, q], sem.at[7, q], at(dc=1))
            cores[q].start()
        for q in order:
            cores[q].wait_recv()
            done(q)
        for q in order:
            own[q][0].wait_send()
            own[q][1].wait_send()
            passed[q].wait_send()
            cores[q].wait_send()

    part = m // NX

    def fetched(ref, d):
        to = lax.rem(z + d, NZ)
        src = ref.at[:, pl.ds(pl.multiple_of(to * m + x * part, part), part), :]
        dst = uk.at[core, pl.ds(4 * z, 4), pl.ds(pl.multiple_of(x * part, part), part), :]
        if d == 0:
            return pltpu.make_async_copy(src, dst, in_s.at[0])
        return remote(src, dst, in_s.at[d], in_r.at[d], at(dz=d))

    for which, ref in ((0, initial), (1, kappa)):

        @pl.when(core == which)
        def _():
            for d in range(NZ):
                fetched(ref, d).start()

    def in_piece(xs, d):
        come = lax.rem(z + NZ - d, NZ)
        return uk.at[core, pl.ds(4 * come, 4), pl.ds(pl.multiple_of(xs * part, part), part), :]

    def in_both(d):
        come = lax.rem(z + NZ - d, NZ)
        return uk.at[core, pl.ds(4 * come, 4)]

    def in_ready(d):
        if d == 0:
            fetched(initial, 0).wait()
        else:
            fetched(initial, d).wait_recv()

    xgather(xi, in_piece, in_both, (0, 1, 7, 2, 6, 3, 5, 4), in_ready, lambda q: None)
    for d in range(1, NZ):
        fetched(initial, d).wait_send()

    def fill(i, _):
        for k in range(4):
            a0[4 + i * 4 + k, pl.ds(0, m)] = uk[0, i * 4 + k]
            kx[4 + i * 4 + k, pl.ds(0, m)] = uk[1, i * 4 + k]
        return 0

    lax.fori_loop(0, n // 4, fill, 0)

    def land():
        for p in list(range(4)) + list(range(n + 4, n + 8)):
            a0[p] = la[p]

        def rows(i, _):
            for k in range(8):
                a0[4 + i * 8 + k, pl.ds(m, 8)] = la[4 + i * 8 + k, pl.ds(m, 8)]
            return 0

        lax.fori_loop(0, n // 8, rows, 0)

    copies = exchange(0, a0, la, 4, n, m, 4) + exchange(4, kx, kx, 4, n, m, 4)
    finish(copies)
    land()

    shift, rowsum = co[8], co[9]

    def first_right(p, here, total):
        lap = total - 6.0 * here
        force = DIFFUSE * lap + REACT * kx[p] * (here - here * here * here)
        f0[p] = here + (rowsum * force - shift * lap)

    sweep_planes(a0, 1, n + 6, 2, first_right)

    def second_right():
        def use(p, here, total):
            own, start = here[:m], p - 4
            lap = total[:m] - 6.0 * own
            force = DIFFUSE * lap + REACT * uk[1, start] * (own - own * own * own)
            fg[core, start // 4, x, lax.rem(start, 4)] = force
            f0[p, pl.ds(0, m)] = uk[0, start] - shift * lap

        sweep_planes(a0, 4, n, 4, use)

        def done(q):
            for k in range(4):
                total = f0[4 + 4 * q + k, pl.ds(0, m)]
                for j in range(2 * NX):
                    total = total + co[j] * fg[j % 2, q, j // 2, k]
                f0[4 + 4 * q + k, pl.ds(0, m)] = total

        xgather(xq, lambda xs, q: fg.at[core, q, xs], lambda q: fg.at[core, q], tuple(range(8)), lambda q: None, done)
        finish(exchange(4, f0, f0, 4, n, m, 4))

    def cycle():
        smooth(a0, b0, f0, co[10], co[11], 1, n + 6, 2)
        smooth(b0, a0, f0, co[10], co[11], 2, n + 4, 2)
        held = []

        def rest0(p, here, total):
            held.append((f0[p] - co[12] * here + co[13] * total)[:m])
            if len(held) == 2:
                i = (p - 5) // 2
                pair = held[0] + held[1]
                rs[0, i], rs[1, i] = pair[:, :128], pair[:, 128:]
                held.clear()

        sweep_planes(a0, 4, n, 2, rest0)

        def pairs0(i, _):
            for k in range(4):
                for h in range(2):
                    cut = pl.ds(128 * h, 128)
                    st[4 * i + k, :, cut] = (
                        rs[h, 4 * i + k, pl.ds(0, m // 2, stride=2)] + rs[h, 4 * i + k, pl.ds(1, m // 2, stride=2)]
                    )
            return 0

        lax.fori_loop(0, n // 8, pairs0, 0)
        coarse = jnp.dot(
            st[...].reshape(n * m // 4, 256), pick0[...], precision=HIGH, preferred_element_type=jnp.float32
        )
        f1[pl.ds(4, n // 2), pl.ds(0, m // 2)] = coarse.reshape(n // 2, m // 2, 128)
        finish(exchange(1, f1, f1, 4, n // 2, m // 2, 2))

        for p in range(2, n // 2 + 6):
            b1[p] = co[14] * f1[p]
        smooth(b1, a1, f1, co[14], co[15], 3, n // 2 + 2, 1)

        def rest1(p, here, total):
            held.append((f1[p] - co[16] * here + co[17] * total)[: m // 2])
            if len(held) == 2:
                rs1[(p - 5) // 2] = held[0] + held[1]
                held.clear()

        sweep_planes(a1, 4, n // 2, 1, rest1)
        for i in range(n // 4):
            st1[i] = rs1[i, pl.ds(0, m // 4, stride=2)] + rs1[i, pl.ds(1, m // 4, stride=2)]
        coarse = jnp.dot(
            st1[...].reshape(n * m // 16, 128), pick1[...], precision=HIGH, preferred_element_type=jnp.float32
        )
        f2[pl.ds(8, n // 4), pl.ds(0, m // 4)] = coarse.reshape(n // 4, m // 4, 128)
        finish(exchange(2, f2, f2, 8, n // 4, m // 4, 8))

        for p in range(n // 4 + 16):
            va[p] = co[18] * f2[p]
        now, later = va, vb
        for k in range(COARSE - 2, -1, -1):
            smooth(now, later, f2, co[18], co[19], 8 - k, n // 4 + 2 * k, 1)
            now, later = later, now

        fine = jnp.dot(
            now[pl.ds(8, n // 4), pl.ds(0, m // 4)].reshape(n * m // 16, 128),
            back1[...],
            precision=HIGH,
            preferred_element_type=jnp.float32,
        ).reshape(n // 4, m // 4, 128)
        for i in range(n // 4):
            w1[i, pl.ds(0, m // 4, stride=2)] = fine[i]
            w1[i, pl.ds(1, m // 4, stride=2)] = fine[i]
        for i in range(n // 4):
            add = w1[i]
            for k in range(2):
                p = 4 + 2 * i + k
                a1[p, pl.ds(0, m // 2)] = a1[p, pl.ds(0, m // 2)] + add
        finish(exchange(3, a1, a1, 4, n // 2, m // 2, 3))
        smooth(a1, b1, f1, co[14], co[15], 2, n // 2 + 4, 1)
        smooth(b1, a1, f1, co[14], co[15], 3, n // 2 + 2, 1)

        xw[...] = jnp.dot(
            a1[pl.ds(3, n // 2 + 2)].reshape((n // 2 + 2) * (m // 2 + 8), 128),
            back0[...],
            precision=HIGH,
            preferred_element_type=jnp.float32,
        ).reshape(n // 2 + 2, m // 2 + 8, 256)

        def widen(i, _):
            for k in range(3):
                g = 3 * i + k
                for h in range(2):
                    cut = pl.ds(128 * h, 128)
                    near = xw[g, pl.ds(0, m // 2 + 2), cut]
                    far = xw[g, pl.ds(m // 2 + 6, 2), cut]
                    for e in range(2):
                        w0[h, g, pl.ds(e, m // 2 + 2, stride=2)] = near
                        w0[h, g, pl.ds(m + 4 + e, 2, stride=2)] = far
                    add = w0[h, g]
                    for e in range(2):
                        a0[2 + 2 * g + e, :, cut] = a0[2 + 2 * g + e, :, cut] + add
            return 0

        lax.fori_loop(0, (n // 2 + 2) // 3, widen, 0)
        smooth(a0, b0, f0, co[10], co[11], 3, n + 2, 2)
        smooth(b0, a0, f0, co[10], co[11], 4, n, 2)

    def turn(v, _):
        @pl.when(v == VCYCLES)
        def _():
            second_right()

        cycle()

        @pl.when(v < SWEEPS * VCYCLES - 1)
        def _():
            finish(exchange(0, a0, la, 4, n, m, 4))
            land()

        return 0

    lax.fori_loop(0, SWEEPS * VCYCLES, turn, 0)

    def sent(d):
        to = lax.rem(z + d, NZ)
        src = a0.at[pl.ds(4 + 4 * to, 4), pl.ds(0, m), :]
        dst = out.at[:, pl.ds(pl.multiple_of(z * m, m), m), :]
        if d == 0:
            return pltpu.make_async_copy(src, dst, out_s.at[0])
        return remote(src, dst, out_s.at[d], out_r.at[d], at(dz=d))

    for d in (4, 3, 5, 2, 6, 1, 7, 0):
        sent(d).start()
    for d in (1, 7, 2, 6, 3, 5, 4):
        sent(d).wait_recv()
    for d in range(1, NZ):
        sent(d).wait_send()
    sent(0).wait()


def per_device(initial, kappa):
    count = lax.axis_size("node")
    assert count == 2 * NX and lax.axis_size("space") == NY * NZ
    thick, rows, cols = initial.shape
    assert thick == 4 and rows == 256 and cols == 256
    n, m = thick * NZ, rows // NZ
    co = jnp.asarray(coefficients(count))[lax.axis_index("node")]
    wide, half = np.arange(cols), np.arange(cols // 2)
    pick0 = np.where(wide[:, None] // 2 == half[None, :], 0.125, 0.0).astype(np.float32)
    pick1 = np.where(half[:, None] // 2 == half[None, :] % (cols // 4), 0.125, 0.0).astype(np.float32)
    back0 = np.where(half[:, None] == wide[None, :] // 2, 1.0, 0.0).astype(np.float32)
    back1 = np.where(half[:, None] == half[None, :] // 2, 1.0, 0.0).astype(np.float32)
    f32 = jnp.float32
    full = pltpu.VMEM((n + 8, m + 8, cols), f32)
    mid = pltpu.VMEM((n // 2 + 8, m // 2 + 8, cols // 2), f32)
    low = pltpu.VMEM((n // 4 + 16, m // 4 + 16, cols // 2), f32)
    dma = pltpu.SemaphoreType.DMA
    vmem = pl.BlockSpec(memory_space=pltpu.VMEM)
    hbm = pl.BlockSpec(memory_space=pl.ANY)
    result = pl.pallas_call(
        kernel,
        out_shape=jax.ShapeDtypeStruct((thick, rows, cols), f32),
        in_specs=[pl.BlockSpec(memory_space=pltpu.SMEM), hbm, hbm, vmem, vmem, vmem, vmem],
        out_specs=hbm,
        scratch_shapes=[
            pltpu.VMEM((2, n, m, cols), f32), full, full, full, full, full,
            pltpu.VMEM((2, 8, NX, n // 8, m, cols), f32),
            pltpu.VMEM((2, n // 2, m, cols // 2), f32), pltpu.VMEM((n // 2, m // 2, cols), f32),
            pltpu.VMEM((2, n // 2 + 2, m + 8, cols // 2), f32), pltpu.VMEM((n // 2 + 2, m // 2 + 8, cols), f32),
            mid, mid, mid,
            pltpu.VMEM((n // 4, m // 2, cols // 2), f32), pltpu.VMEM((n // 4, m // 4, cols // 2), f32),
            pltpu.VMEM((n // 4, m // 2, cols // 2), f32),
            low, low, low,
            dma((NZ,)), dma((NZ,)), dma((8, NZ)), dma((8, NZ)), dma((5, 8)), dma((5, 8)), dma((NZ,)), dma((NZ,)),
        ],
        compiler_params=pltpu.CompilerParams(collective_id=0, has_side_effects=True, vmem_limit_bytes=60 * 2**20),
    )(co, initial, kappa, jnp.asarray(pick0), jnp.asarray(pick1), jnp.asarray(back0), jnp.asarray(back1))
    return result[None]


def solution(mesh):
    slab = P("space", None, None)
    return jax.shard_map(
        per_device, mesh=mesh, in_specs=(slab, slab), out_specs=P("node", "space", None, None), check_vma=False
    )
```

profile of v0, /device:TPU:2, one launch (start us, length us, event | category | flops | bytes accessed | tf_op | source)
XLA Modules:
  0.0 208.3 jit_solution(8410987015629912899)
XLA Ops:
  0.0 1.2 dynamic-slice_bitcast_fusion.co
  1.2 204.8 %shard_map.73 = f32[4,256,256]{2,1,0:T(8,128)} custom-call(f32[24]{0:T(128)} %dynamic-slice_bitcast_fusion.co, f32[4,256,256]{2,1,0:T(8,128)} %initial.1, f32[4,256,256]{2,1,0:T(8,128)} %kappa.1, f32[256,128]{1,0:T(8,128)} %constant.21.clone.pick0, f32[128,128]{1,0:T(8,128)} %constant.22.clone.pick1, f32[128,256]{1,0:T(8,128)} %constant.23.clone.back0, ...), custom_call_target="tpu_custom_call" | custom-call | tf_op jit(solution)/shard_map/pallas_call | solution.py:464
  206.0 2.3 %copy.9 = f32[1,4,256,256]{3,2,1,0:T(8,128)} copy(f32[1,4,256,256]{3,2,1,0:T(8,128)} %bitcast.3) | data formatting | bytes 2097152
where the time goes:
time: 210 us; the launch traced here: 208 us
  Pallas kernels  205 us (98%)
  local copies, waits for them, and re-layouts  3.49 us (2%)
    pallas_call x1, Pallas kernels, per_device(): pl.pallas_call(kernel, out_shape=jax.ShapeDtypeStruct((thick, rows, cols)...  205 us

commit v1 on v0

--- a/solution.py
+++ b/solution.py
@@ -15,7 +15,7 @@
 REACT = 0.5
 OMEGA = 0.8
 MESH = pl.DeviceIdType.MESH
-HIGH = lax.Precision.HIGHEST
+ROW = 24
 
 NY = 4
 NZ = 8
@@ -91,8 +91,8 @@
             s = shift / 4.0**level
             a = OMEGA / (1.0 + 6.0 * s)
             row += [a, a * s, 1.0 + 6.0 * s, s]
-        rows.append(row + [0.0] * (24 - len(row)))
-    return np.asarray(rows, np.float32)
+        rows.append(row + [0.0] * (ROW - len(row)))
+    return np.asarray(rows, np.float32).reshape(-1)
 
 
 def sides(c):
@@ -128,17 +128,28 @@
     sweep_planes(src, first, count, parts, use)
 
 
+def choose(left, right):
+    total = None
+    for _ in range(3):
+        piece = left.astype(jnp.bfloat16)
+        left = left - piece.astype(jnp.float32)
+        term = jnp.dot(piece, right, preferred_element_type=jnp.float32)
+        total = term if total is None else total + term
+    return total
+
+
 def kernel(
-    co, initial, kappa, pick0, pick1, back0, back1, out,
-    uk, a0, b0, f0, la, kx, fg, rs, st, w0, xw,
-    a1, b1, f1, rs1, st1, w1, f2, va, vb,
-    in_s, in_r, xi, xq, halo_s, halo_r, out_s, out_r,
+    table, initial, kappa, out,
+    uk, a0, b0, f0, la, fg, sums, come, rs, st, w0, xw,
+    a1, b1, f1, rs1, st1, w1, pk, f2, va, vb, pick0, pick1, back0, back1,
+    in_s, in_r, xi, xq, halo_s, halo_r, rows_s, rows_r, out_s, out_r,
 ):
     node = lax.axis_index("node")
     space = lax.axis_index("space")
     x, core = node // 2, lax.rem(node, 2)
     y, z = space // NZ, lax.rem(space, NZ)
     n, m = NZ * 4, a0.shape[1] - 8
+    co = [table[node * ROW + i] for i in range(20)]
 
     def at(dx=0, dc=0, dy=0, dz=0):
         nx = lax.rem(x + dx + NX, NX)
@@ -160,20 +171,20 @@
             src_ref=src, dst_ref=dst, send_sem=send, recv_sem=recv, device_id=device, device_id_type=MESH
         )
 
-    def exchange(kind, src, dst, origin, planes, rows, width):
-        total = src.shape[1]
-
-        def span(step, size, start, wrap):
-            if step == 0:
-                return pl.ds(start, size), pl.ds(start, size)
-            if step < 0:
-                return pl.ds(start, width), pl.ds(start + size, width)
-            return pl.ds(start + size - width, width), pl.ds(wrap, width)
-
+    def span(step, size, start, wrap, width):
+        if step == 0:
+            return pl.ds(start, size), pl.ds(start, size)
+        if step < 0:
+            return pl.ds(start, width), pl.ds(start + size, width)
+        return pl.ds(start + size - width, width), pl.ds(wrap, width)
+
+    def exchange(kind, src, dst, origin, planes, rows, total, width, wide, dirs=DIRS):
         copies = []
         for d, (a, b) in enumerate(DIRS):
-            ps, pd = span(a, planes, origin, origin - width)
-            qs, qd = span(b, rows, 0, total - width)
+            if (a, b) not in dirs:
+                continue
+            ps, pd = span(a, planes, origin, origin - width, width)
+            qs, qd = span(b, rows, 0, total - wide, wide)
             copies.append(
                 remote(src.at[ps, qs], dst.at[pd, qd], halo_s.at[kind, d], halo_r.at[kind, d], at(dy=a, dz=b))
             )
@@ -187,46 +198,12 @@
         for copy in copies:
             copy.wait_send()
 
-    def xgather(sem, piece, both, order, ready, done):
-        own = {}
-        for q in order:
-            ready(q)
-            own[q] = [
-                remote(piece(x, q), piece(x, q), sem.at[0, q], sem.at[1, q], at(dx=1)),
-                remote(piece(x, q), piece(x, q), sem.at[2, q], sem.at[3, q], at(dx=-1)),
-            ]
-            for copy in own[q]:
-                copy.start()
-        left, right = lax.rem(x + NX - 1, NX), lax.rem(x + 1, NX)
-        passed, cores = {}, {}
-        for q in order:
-            own[q][0].wait_recv()
-            if q % 2 == 0:
-                passed[q] = remote(piece(left, q), piece(left, q), sem.at[4, q], sem.at[5, q], at(dx=1))
-                passed[q].start()
-            own[q][1].wait_recv()
-            if q % 2 == 1:
-                passed[q] = remote(piece(right, q), piece(right, q), sem.at[4, q], sem.at[5, q], at(dx=-1))
-                passed[q].start()
-        for q in order:
-            passed[q].wait_recv()
-            cores[q] = remote(both(q), both(q), sem.at[6, q], sem.at[7, q], at(dc=1))
-            cores[q].start()
-        for q in order:
-            cores[q].wait_recv()
-            done(q)
-        for q in order:
-            own[q][0].wait_send()
-            own[q][1].wait_send()
-            passed[q].wait_send()
-            cores[q].wait_send()
-
     part = m // NX
 
     def fetched(ref, d):
         to = lax.rem(z + d, NZ)
         src = ref.at[:, pl.ds(pl.multiple_of(to * m + x * part, part), part), :]
-        dst = uk.at[core, pl.ds(4 * z, 4), pl.ds(pl.multiple_of(x * part, part), part), :]
+        dst = uk.at[core, pl.ds(4 + 4 * z, 4), pl.ds(pl.multiple_of(x * part, part), part), :]
         if d == 0:
             return pltpu.make_async_copy(src, dst, in_s.at[0])
         return remote(src, dst, in_s.at[d], in_r.at[d], at(dz=d))
@@ -238,31 +215,77 @@
             for d in range(NZ):
                 fetched(ref, d).start()
 
+    def made(ref, test, value):
+        i = lax.broadcasted_iota(jnp.int32, ref.shape, 0)
+        j = lax.broadcasted_iota(jnp.int32, ref.shape, 1)
+        ref[...] = jnp.where(test(i, j), value, 0.0).astype(jnp.bfloat16)
+
+    made(pick0, lambda i, j: lax.shift_right_logical(i, 1) == j, 0.125)
+    made(pick1, lambda i, j: lax.shift_right_logical(i, 1) == jnp.bitwise_and(j, 63), 0.125)
+    made(back0, lambda i, j: i == lax.shift_right_logical(j, 1), 1.0)
+    made(back1, lambda i, j: i == lax.shift_right_logical(j, 1), 1.0)
+
     def in_piece(xs, d):
-        come = lax.rem(z + NZ - d, NZ)
-        return uk.at[core, pl.ds(4 * come, 4), pl.ds(pl.multiple_of(xs * part, part), part), :]
+        first = 4 + 4 * lax.rem(z + NZ - d, NZ)
+        return uk.at[core, pl.ds(first, 4), pl.ds(pl.multiple_of(xs * part, part), part)]
 
     def in_both(d):
-        come = lax.rem(z + NZ - d, NZ)
-        return uk.at[core, pl.ds(4 * come, 4)]
-
-    def in_ready(d):
-        if d == 0:
-            fetched(initial, 0).wait()
+        return uk.at[core, pl.ds(4 + 4 * lax.rem(z + NZ - d, NZ), 4), pl.ds(0, m)]
+
+    order = (0, 1, 7, 2, 6, 3, 5, 4)
+    left, right = lax.rem(x + NX - 1, NX), lax.rem(x + 1, NX)
+    own, passed, cores = {}, {}, {}
+    for q in order:
+        if q == 0:
+            fetched(initial, q).wait()
         else:
-            fetched(initial, d).wait_recv()
-
-    xgather(xi, in_piece, in_both, (0, 1, 7, 2, 6, 3, 5, 4), in_ready, lambda q: None)
+            fetched(initial, q).wait_recv()
+        own[q] = [
+            remote(in_piece(x, q), in_piece(x, q), xi.at[0, q], xi.at[1, q], at(dx=1)),
+            remote(in_piece(x, q), in_piece(x, q), xi.at[2, q], xi.at[3, q], at(dx=-1)),
+        ]
+        for copy in own[q]:
+            copy.start()
+    for q in order:
+        own[q][0].wait_recv()
+        if q % 2 == 0:
+            passed[q] = remote(in_piece(left, q), in_piece(left, q), xi.at[4, q], xi.at[5, q], at(dx=1))
+            passed[q].start()
+        own[q][1].wait_recv()
+        if q % 2 == 1:
+            passed[q] = remote(in_piece(right, q), in_piece(right, q), xi.at[4, q], xi.at[5, q], at(dx=-1))
+            passed[q].start()
+    for q in order:
+        passed[q].wait_recv()
+        cores[q] = remote(in_both(q), in_both(q), xi.at[6, q], xi.at[7, q], at(dc=1))
+        cores[q].start()
+    mine = uk.at[core]
+    finish(exchange(0, mine, mine, 4, n, m, m + 8, 4, 4))
+    edges = [
+        uk.at[core, pl.ds(0, 4)],
+        uk.at[core, pl.ds(n + 4, 4)],
+        uk.at[core, pl.ds(4, n), pl.ds(m, 8)],
+    ]
+    given = [remote(e, e, rows_s.at[0, i], rows_r.at[0, i], at(dc=1)) for i, e in enumerate(edges)]
+    for copy in given:
+        copy.start()
+    for q in order:
+        cores[q].wait_recv()
+    finish(given)
+    for q in order:
+        own[q][0].wait_send()
+        own[q][1].wait_send()
+        passed[q].wait_send()
+        cores[q].wait_send()
     for d in range(1, NZ):
         fetched(initial, d).wait_send()
 
     def fill(i, _):
         for k in range(4):
-            a0[4 + i * 4 + k, pl.ds(0, m)] = uk[0, i * 4 + k]
-            kx[4 + i * 4 + k, pl.ds(0, m)] = uk[1, i * 4 + k]
+            a0[i * 4 + k] = uk[0, i * 4 + k]
         return 0
 
-    lax.fori_loop(0, n // 4, fill, 0)
+    lax.fori_loop(0, (n + 8) // 4, fill, 0)
 
     def land():
         for p in list(range(4)) + list(range(n + 4, n + 8)):
@@ -275,38 +298,93 @@
 
         lax.fori_loop(0, n // 8, rows, 0)
 
-    copies = exchange(0, a0, la, 4, n, m, 4) + exchange(4, kx, kx, 4, n, m, 4)
-    finish(copies)
-    land()
-
     shift, rowsum = co[8], co[9]
 
     def first_right(p, here, total):
         lap = total - 6.0 * here
-        force = DIFFUSE * lap + REACT * kx[p] * (here - here * here * here)
+        force = DIFFUSE * lap + REACT * uk[1, p] * (here - here * here * here)
         f0[p] = here + (rowsum * force - shift * lap)
 
     sweep_planes(a0, 1, n + 6, 2, first_right)
 
     def second_right():
-        def use(p, here, total):
-            own, start = here[:m], p - 4
-            lap = total[:m] - 6.0 * own
-            force = DIFFUSE * lap + REACT * uk[1, start] * (own - own * own * own)
-            fg[core, start // 4, x, lax.rem(start, 4)] = force
-            f0[p, pl.ds(0, m)] = uk[0, start] - shift * lap
-
-        sweep_planes(a0, 4, n, 4, use)
-
-        def done(q):
+        def toward(q):
+            step = 1 - 2 * lax.rem(x, 2)
+            return step if q < 4 else -step
+
+        def sent_pair(q, dx):
+            return remote(fg.at[0, core, q], fg.at[1, core, q], xq.at[0, q], xq.at[1, q], at(dx=dx))
+
+        def sent_core(pair, q):
+            ref = fg.at[pair, core, q]
+            return remote(ref, ref, xq.at[2 + 2 * pair, q], xq.at[3 + 2 * pair, q], at(dc=1))
+
+        def sent_cross(q):
+            return remote(sums.at[q], come.at[q], xq.at[6, q], xq.at[7, q], at(dx=-toward(q)))
+
+        def forces(i, _):
+            for h in range(2):
+                q = 4 * h + i
+
+                def use(p, here, total):
+                    own = here[:m]
+                    lap = total[:m] - 6.0 * own
+                    force = DIFFUSE * lap + REACT * uk[1, p, pl.ds(0, m)] * (own - own * own * own)
+                    fg[0, core, q, p - 4 * q - 4] = force
+                    f0[p, pl.ds(0, m)] = uk[0, p, pl.ds(0, m)] - shift * lap
+
+                sweep_planes(a0, 4 + 4 * q, 4, 1, use)
+                sent_pair(q, toward(4 * h)).start()
+                sent_core(0, q).start()
+            return 0
+
+        lax.fori_loop(0, 4, forces, 0)
+
+        def gathered(q):
+            sent_core(0, q).wait_recv()
+            sent_core(1, q).wait_recv()
+            there = lax.rem(x + toward(q) + NX, NX)
+            cross = lax.rem(x - toward(q) + NX, NX)
+            nodes = [(e, c, 2 * (x if e == 0 else there) + c) for e in (0, 1) for c in (0, 1)]
             for k in range(4):
-                total = f0[4 + 4 * q + k, pl.ds(0, m)]
-                for j in range(2 * NX):
-                    total = total + co[j] * fg[j % 2, q, j // 2, k]
-                f0[4 + 4 * q + k, pl.ds(0, m)] = total
-
-        xgather(xq, lambda xs, q: fg.at[core, q, xs], lambda q: fg.at[core, q], tuple(range(8)), lambda q: None, done)
-        finish(exchange(4, f0, f0, 4, n, m, 4))
+                forth, keep = None, f0[4 + 4 * q + k, pl.ds(0, m)]
+                for e, c, j in nodes:
+                    force = fg[e, c, q, k]
+                    term = table[(2 * cross + core) * ROW + j] * force
+                    forth = term if forth is None else forth + term
+                    keep = keep + table[node * ROW + j] * force
+                sums[q, k] = forth
+                f0[4 + 4 * q + k, pl.ds(0, m)] = keep
+            sent_cross(q).start()
+
+        order = (0, 4, 1, 5, 2, 6, 3, 7)
+        last = None
+        for q in order:
+            sent_pair(q, toward(q)).wait_recv()
+            sent_core(1, q).start()
+            if last is not None:
+                gathered(last)
+            last = q
+        gathered(last)
+        faces = []
+        for q in order:
+            sent_cross(q).wait_recv()
+            for k in range(4):
+                f0[4 + 4 * q + k, pl.ds(0, m)] = f0[4 + 4 * q + k, pl.ds(0, m)] + come[q, k]
+            ps = pl.ds(4 + 4 * q, 4)
+            for i, b in enumerate((-1, 1)):
+                qs, qd = span(b, m, 0, m + 4, 4)
+                faces.append(remote(f0.at[ps, qs], f0.at[ps, qd], rows_s.at[i, q], rows_r.at[i, q], at(dz=b)))
+                faces[-1].start()
+            if q in (0, 7):
+                a = -1 if q == 0 else 1
+                faces += exchange(4, f0, f0, 4, n, m, m + 8, 4, 4, [(a, b) for b in (-1, 0, 1)])
+        finish(faces)
+        for q in order:
+            sent_pair(q, toward(q)).wait_send()
+            sent_core(0, q).wait_send()
+            sent_core(1, q).wait_send()
+            sent_cross(q).wait_send()
 
     def cycle():
         smooth(a0, b0, f0, co[10], co[11], 1, n + 6, 2)
@@ -333,11 +411,9 @@
             return 0
 
         lax.fori_loop(0, n // 8, pairs0, 0)
-        coarse = jnp.dot(
-            st[...].reshape(n * m // 4, 256), pick0[...], precision=HIGH, preferred_element_type=jnp.float32
-        )
+        coarse = choose(st[...].reshape(n * m // 4, 256), pick0[...])
         f1[pl.ds(4, n // 2), pl.ds(0, m // 2)] = coarse.reshape(n // 2, m // 2, 128)
-        finish(exchange(1, f1, f1, 4, n // 2, m // 2, 2))
+        finish(exchange(1, f1, f1, 4, n // 2, m // 2, m // 2 + 8, 2, 2))
 
         for p in range(2, n // 2 + 6):
             b1[p] = co[14] * f1[p]
@@ -352,25 +428,26 @@
         sweep_planes(a1, 4, n // 2, 1, rest1)
         for i in range(n // 4):
             st1[i] = rs1[i, pl.ds(0, m // 4, stride=2)] + rs1[i, pl.ds(1, m // 4, stride=2)]
-        coarse = jnp.dot(
-            st1[...].reshape(n * m // 16, 128), pick1[...], precision=HIGH, preferred_element_type=jnp.float32
-        )
-        f2[pl.ds(8, n // 4), pl.ds(0, m // 4)] = coarse.reshape(n // 4, m // 4, 128)
-        finish(exchange(2, f2, f2, 8, n // 4, m // 4, 8))
-
-        for p in range(n // 4 + 16):
-            va[p] = co[18] * f2[p]
+        coarse = choose(st1[...].reshape(n * m // 16, 128), pick1[...]).reshape(n // 4, m // 4, 128)
+        low = lax.broadcasted_iota(jnp.int32, (m // 4, 128), 1) < 64
+        for i in range(n // 8):
+            pk[4 + i, pl.ds(0, m // 4)] = jnp.where(low, coarse[2 * i], coarse[2 * i + 1])
+        finish(exchange(2, pk, pk, 4, n // 8, m // 4, m // 4 + 16, 4, 8))
+
+        low = lax.broadcasted_iota(jnp.int32, (m // 4 + 16, 128), 1) < 64
+        for i in range(n // 8 + 8):
+            here = pk[i]
+            turned = pltpu.roll(here, 64, 1)
+            for k, value in ((0, jnp.where(low, here, turned)), (1, jnp.where(low, turned, here))):
+                f2[2 * i + k] = value
+                va[2 * i + k] = co[18] * value
         now, later = va, vb
         for k in range(COARSE - 2, -1, -1):
             smooth(now, later, f2, co[18], co[19], 8 - k, n // 4 + 2 * k, 1)
             now, later = later, now
 
-        fine = jnp.dot(
-            now[pl.ds(8, n // 4), pl.ds(0, m // 4)].reshape(n * m // 16, 128),
-            back1[...],
-            precision=HIGH,
-            preferred_element_type=jnp.float32,
-        ).reshape(n // 4, m // 4, 128)
+        fine = choose(now[pl.ds(8, n // 4), pl.ds(0, m // 4)].reshape(n * m // 16, 128), back1[...])
+        fine = fine.reshape(n // 4, m // 4, 128)
         for i in range(n // 4):
             w1[i, pl.ds(0, m // 4, stride=2)] = fine[i]
             w1[i, pl.ds(1, m // 4, stride=2)] = fine[i]
@@ -379,16 +456,12 @@
             for k in range(2):
                 p = 4 + 2 * i + k
                 a1[p, pl.ds(0, m // 2)] = a1[p, pl.ds(0, m // 2)] + add
-        finish(exchange(3, a1, a1, 4, n // 2, m // 2, 3))
+        finish(exchange(3, a1, a1, 4, n // 2, m // 2, m // 2 + 8, 3, 3))
         smooth(a1, b1, f1, co[14], co[15], 2, n // 2 + 4, 1)
         smooth(b1, a1, f1, co[14], co[15], 3, n // 2 + 2, 1)
 
-        xw[...] = jnp.dot(
-            a1[pl.ds(3, n // 2 + 2)].reshape((n // 2 + 2) * (m // 2 + 8), 128),
-            back0[...],
-            precision=HIGH,
-            preferred_element_type=jnp.float32,
-        ).reshape(n // 2 + 2, m // 2 + 8, 256)
+        fine = choose(a1[pl.ds(3, n // 2 + 2)].reshape((n // 2 + 2) * (m // 2 + 8), 128), back0[...])
+        xw[...] = fine.reshape(n // 2 + 2, m // 2 + 8, 256)
 
         def widen(i, _):
             for k in range(3):
@@ -418,7 +491,7 @@
 
         @pl.when(v < SWEEPS * VCYCLES - 1)
         def _():
-            finish(exchange(0, a0, la, 4, n, m, 4))
+            finish(exchange(0, a0, la, 4, n, m, m + 8, 4, 4))
             land()
 
         return 0
@@ -448,37 +521,34 @@
     thick, rows, cols = initial.shape
     assert thick == 4 and rows == 256 and cols == 256
     n, m = thick * NZ, rows // NZ
-    co = jnp.asarray(coefficients(count))[lax.axis_index("node")]
-    wide, half = np.arange(cols), np.arange(cols // 2)
-    pick0 = np.where(wide[:, None] // 2 == half[None, :], 0.125, 0.0).astype(np.float32)
-    pick1 = np.where(half[:, None] // 2 == half[None, :] % (cols // 4), 0.125, 0.0).astype(np.float32)
-    back0 = np.where(half[:, None] == wide[None, :] // 2, 1.0, 0.0).astype(np.float32)
-    back1 = np.where(half[:, None] == half[None, :] // 2, 1.0, 0.0).astype(np.float32)
     f32 = jnp.float32
     full = pltpu.VMEM((n + 8, m + 8, cols), f32)
     mid = pltpu.VMEM((n // 2 + 8, m // 2 + 8, cols // 2), f32)
     low = pltpu.VMEM((n // 4 + 16, m // 4 + 16, cols // 2), f32)
     dma = pltpu.SemaphoreType.DMA
-    vmem = pl.BlockSpec(memory_space=pltpu.VMEM)
+    chunks = pltpu.VMEM((8, n // 8, m, cols), f32)
+    pick = lambda i, j: pltpu.VMEM((i, j), jnp.bfloat16)
     hbm = pl.BlockSpec(memory_space=pl.ANY)
     result = pl.pallas_call(
         kernel,
         out_shape=jax.ShapeDtypeStruct((thick, rows, cols), f32),
-        in_specs=[pl.BlockSpec(memory_space=pltpu.SMEM), hbm, hbm, vmem, vmem, vmem, vmem],
+        in_specs=[pl.BlockSpec(memory_space=pltpu.SMEM), hbm, hbm],
         out_specs=hbm,
         scratch_shapes=[
-            pltpu.VMEM((2, n, m, cols), f32), full, full, full, full, full,
-            pltpu.VMEM((2, 8, NX, n // 8, m, cols), f32),
+            pltpu.VMEM((2, n + 8, m + 8, cols), f32), full, full, full, full,
+            pltpu.VMEM((2, 2, 8, n // 8, m, cols), f32), chunks, chunks,
             pltpu.VMEM((2, n // 2, m, cols // 2), f32), pltpu.VMEM((n // 2, m // 2, cols), f32),
             pltpu.VMEM((2, n // 2 + 2, m + 8, cols // 2), f32), pltpu.VMEM((n // 2 + 2, m // 2 + 8, cols), f32),
             mid, mid, mid,
             pltpu.VMEM((n // 4, m // 2, cols // 2), f32), pltpu.VMEM((n // 4, m // 4, cols // 2), f32),
             pltpu.VMEM((n // 4, m // 2, cols // 2), f32),
-            low, low, low,
-            dma((NZ,)), dma((NZ,)), dma((8, NZ)), dma((8, NZ)), dma((5, 8)), dma((5, 8)), dma((NZ,)), dma((NZ,)),
+            pltpu.VMEM((n // 8 + 8, m // 4 + 16, cols // 2), f32), low, low, low,
+            pick(cols, cols // 2), pick(cols // 2, cols // 2), pick(cols // 2, cols), pick(cols // 2, cols // 2),
+            dma((NZ,)), dma((NZ,)), dma((8, NZ)), dma((8, NZ)), dma((5, 8)), dma((5, 8)), dma((2, 8)), dma((2, 8)),
+            dma((NZ,)), dma((NZ,)),
         ],
         compiler_params=pltpu.CompilerParams(collective_id=0, has_side_effects=True, vmem_limit_bytes=60 * 2**20),
-    )(co, initial, kappa, jnp.asarray(pick0), jnp.asarray(pick1), jnp.asarray(back0), jnp.asarray(back1))
+    )(jnp.asarray(coefficients(count)), initial, kappa)
     return result[None]
 
 

time: 210 us -> 185 us (0.88)
  Pallas kernels: 205 us -> 182 us
    pallas_call x1, Pallas kernels: 205 us -> 182 us  [per_device(): pl.pallas_call(kernel, out_shape=jax.ShapeDtypeStruct((thick, rows, cols)...]
where the time goes in v1:
time: 185 us
  Pallas kernels  182 us (98%)
  local copies, waits for them, and re-layouts  2.29 us (1%)
    pallas_call x1, Pallas kernels, per_device(): pl.pallas_call(kernel, out_shape=jax.ShapeDtypeStruct((thick, rows, cols)...  182 us

profile of v1, /device:TPU:2, one launch (start us, length us, event | category | flops | bytes accessed | tf_op | source)
XLA Modules:
  0.0 184.6 jit_solution(9072530190198599882)
XLA Ops:
  0.0 182.3 %shard_map.37 = f32[4,256,256]{2,1,0:T(8,128)} custom-call(f32[192]{0:T(256)} %constant.2.clone.table, f32[4,256,256]{2,1,0:T(8,128)} %initial.1, f32[4,256,256]{2,1,0:T(8,128)} %kappa.1), custom_call_target="tpu_custom_call" | custom-call | tf_op jit(solution)/shard_map/pallas_call | solution.py:532
  182.3 2.3 %copy.5 = f32[1,4,256,256]{3,2,1,0:T(8,128)} copy(f32[1,4,256,256]{3,2,1,0:T(8,128)} %bitcast.1) | data formatting | bytes 2097152

commit v2 on v1

--- a/solution.py
+++ b/solution.py
@@ -98,6 +98,9 @@
 def sides(c):
     r, l = c.shape
     total = pltpu.roll(c, 1, 0) + pltpu.roll(c, r - 1, 0)
+    if l == 256:
+        even, odd = c[:, :128], c[:, 128:]
+        return total + jnp.concatenate([odd + pltpu.roll(odd, 1, 1), even + pltpu.roll(even, 127, 1)], axis=1)
     return total + (pltpu.roll(c, 1, 1) + pltpu.roll(c, l - 1, 1))
 
 
@@ -121,9 +124,9 @@
         lax.fori_loop(0, parts, part, 0)
 
 
-def smooth(src, dst, f, a, b, first, count, parts):
+def smooth(src, dst, f, b, first, count, parts):
     def use(p, here, total):
-        dst[p] = (1.0 - OMEGA) * here + (a * f[p] + b * total)
+        dst[p] = (1.0 - OMEGA) * here + (f[p] + b * total)
 
     sweep_planes(src, first, count, parts, use)
 
@@ -140,9 +143,9 @@
 
 def kernel(
     table, initial, kappa, out,
-    uk, a0, b0, f0, la, fg, sums, come, rs, st, w0, xw,
-    a1, b1, f1, rs1, st1, w1, pk, f2, va, vb, pick0, pick1, back0, back1,
-    in_s, in_r, xi, xq, halo_s, halo_r, rows_s, rows_r, out_s, out_r,
+    uk, a0, b0, f0, la, fg, sums, come, ready, rs, w0,
+    a1, b1, f1, rs1, st1, w1, pk, f2, va, vb, apart, joined, pick1, back1,
+    in_s, in_r, xi, xq, halo_s, halo_r, rows_s, rows_r, side_s, side_r, out_s, out_r,
 ):
     node = lax.axis_index("node")
     space = lax.axis_index("space")
@@ -178,7 +181,7 @@
             return pl.ds(start, width), pl.ds(start + size, width)
         return pl.ds(start + size - width, width), pl.ds(wrap, width)
 
-    def exchange(kind, src, dst, origin, planes, rows, total, width, wide, dirs=DIRS):
+    def exchange(kind, src, dst, origin, planes, rows, total, width, wide, dirs=DIRS, start=True):
         copies = []
         for d, (a, b) in enumerate(DIRS):
             if (a, b) not in dirs:
@@ -188,8 +191,9 @@
             copies.append(
                 remote(src.at[ps, qs], dst.at[pd, qd], halo_s.at[kind, d], halo_r.at[kind, d], at(dy=a, dz=b))
             )
-        for copy in copies:
-            copy.start()
+        if start:
+            for copy in copies:
+                copy.start()
         return copies
 
     def finish(copies):
@@ -220,9 +224,10 @@
         j = lax.broadcasted_iota(jnp.int32, ref.shape, 1)
         ref[...] = jnp.where(test(i, j), value, 0.0).astype(jnp.bfloat16)
 
-    made(pick0, lambda i, j: lax.shift_right_logical(i, 1) == j, 0.125)
+    half = m * NZ // 2
+    made(apart, lambda i, j: i == jnp.where(j < half, 2 * j, 2 * (j - half) + 1), 1.0)
+    made(joined, lambda i, j: j == jnp.where(i < half, 2 * i, 2 * (i - half) + 1), 1.0)
     made(pick1, lambda i, j: lax.shift_right_logical(i, 1) == jnp.bitwise_and(j, 63), 0.125)
-    made(back0, lambda i, j: i == lax.shift_right_logical(j, 1), 1.0)
     made(back1, lambda i, j: i == lax.shift_right_logical(j, 1), 1.0)
 
     def in_piece(xs, d):
@@ -240,6 +245,8 @@
             fetched(initial, q).wait()
         else:
             fetched(initial, q).wait_recv()
+        here = in_piece(x, q)
+        here[...] = choose(here[...].reshape(4 * part, 2 * half), apart[...]).reshape(4, part, 2 * half)
         own[q] = [
             remote(in_piece(x, q), in_piece(x, q), xi.at[0, q], xi.at[1, q], at(dx=1)),
             remote(in_piece(x, q), in_piece(x, q), xi.at[2, q], xi.at[3, q], at(dx=-1)),
@@ -287,23 +294,12 @@
 
     lax.fori_loop(0, (n + 8) // 4, fill, 0)
 
-    def land():
-        for p in list(range(4)) + list(range(n + 4, n + 8)):
-            a0[p] = la[p]
-
-        def rows(i, _):
-            for k in range(8):
-                a0[4 + i * 8 + k, pl.ds(m, 8)] = la[4 + i * 8 + k, pl.ds(m, 8)]
-            return 0
-
-        lax.fori_loop(0, n // 8, rows, 0)
-
     shift, rowsum = co[8], co[9]
 
     def first_right(p, here, total):
         lap = total - 6.0 * here
         force = DIFFUSE * lap + REACT * uk[1, p] * (here - here * here * here)
-        f0[p] = here + (rowsum * force - shift * lap)
+        f0[p] = co[10] * (here + (rowsum * force - shift * lap))
 
     sweep_planes(a0, 1, n + 6, 2, first_right)
 
@@ -331,7 +327,7 @@
                     lap = total[:m] - 6.0 * own
                     force = DIFFUSE * lap + REACT * uk[1, p, pl.ds(0, m)] * (own - own * own * own)
                     fg[0, core, q, p - 4 * q - 4] = force
-                    f0[p, pl.ds(0, m)] = uk[0, p, pl.ds(0, m)] - shift * lap
+                    f0[p, pl.ds(0, m)] = co[10] * (uk[0, p, pl.ds(0, m)] - shift * lap)
 
                 sweep_planes(a0, 4 + 4 * q, 4, 1, use)
                 sent_pair(q, toward(4 * h)).start()
@@ -350,9 +346,9 @@
                 forth, keep = None, f0[4 + 4 * q + k, pl.ds(0, m)]
                 for e, c, j in nodes:
                     force = fg[e, c, q, k]
-                    term = table[(2 * cross + core) * ROW + j] * force
+                    term = (table[(2 * cross + core) * ROW + j] * table[(2 * cross + core) * ROW + 10]) * force
                     forth = term if forth is None else forth + term
-                    keep = keep + table[node * ROW + j] * force
+                    keep = keep + (table[node * ROW + j] * co[10]) * force
                 sums[q, k] = forth
                 f0[4 + 4 * q + k, pl.ds(0, m)] = keep
             sent_cross(q).start()
@@ -386,48 +382,38 @@
             sent_core(1, q).wait_send()
             sent_cross(q).wait_send()
 
-    def cycle():
-        smooth(a0, b0, f0, co[10], co[11], 1, n + 6, 2)
-        smooth(b0, a0, f0, co[10], co[11], 2, n + 4, 2)
+    def cycle(v):
+        smooth(b0, a0, f0, co[11], 2, n + 4, 1)
         held = []
 
         def rest0(p, here, total):
-            held.append((f0[p] - co[12] * here + co[13] * total)[:m])
+            held.append((f0[p] - OMEGA * here + co[11] * total)[:m])
             if len(held) == 2:
-                i = (p - 5) // 2
                 pair = held[0] + held[1]
-                rs[0, i], rs[1, i] = pair[:, :128], pair[:, 128:]
+                rs[(p - 5) // 2] = pair[:, :128] + pair[:, 128:]
                 held.clear()
 
-        sweep_planes(a0, 4, n, 2, rest0)
-
-        def pairs0(i, _):
-            for k in range(4):
-                for h in range(2):
-                    cut = pl.ds(128 * h, 128)
-                    st[4 * i + k, :, cut] = (
-                        rs[h, 4 * i + k, pl.ds(0, m // 2, stride=2)] + rs[h, 4 * i + k, pl.ds(1, m // 2, stride=2)]
-                    )
-            return 0
-
-        lax.fori_loop(0, n // 8, pairs0, 0)
-        coarse = choose(st[...].reshape(n * m // 4, 256), pick0[...])
-        f1[pl.ds(4, n // 2), pl.ds(0, m // 2)] = coarse.reshape(n // 2, m // 2, 128)
+        sweep_planes(a0, 4, n, 1, rest0)
+        mean = 0.125 * co[14] / co[10]
+        for i in range(n // 2):
+            f1[4 + i, pl.ds(0, m // 2)] = mean * (
+                rs[i, pl.ds(0, m // 2, stride=2)] + rs[i, pl.ds(1, m // 2, stride=2)]
+            )
         finish(exchange(1, f1, f1, 4, n // 2, m // 2, m // 2 + 8, 2, 2))
 
-        for p in range(2, n // 2 + 6):
-            b1[p] = co[14] * f1[p]
-        smooth(b1, a1, f1, co[14], co[15], 3, n // 2 + 2, 1)
+        smooth(f1, a1, f1, co[15], 3, n // 2 + 2, 1)
 
         def rest1(p, here, total):
-            held.append((f1[p] - co[16] * here + co[17] * total)[: m // 2])
+            held.append((f1[p] - OMEGA * here + co[15] * total)[: m // 2])
             if len(held) == 2:
                 rs1[(p - 5) // 2] = held[0] + held[1]
                 held.clear()
 
         sweep_planes(a1, 4, n // 2, 1, rest1)
         for i in range(n // 4):
-            st1[i] = rs1[i, pl.ds(0, m // 4, stride=2)] + rs1[i, pl.ds(1, m // 4, stride=2)]
+            st1[i] = (co[18] / co[14]) * (
+                rs1[i, pl.ds(0, m // 4, stride=2)] + rs1[i, pl.ds(1, m // 4, stride=2)]
+            )
         coarse = choose(st1[...].reshape(n * m // 16, 128), pick1[...]).reshape(n // 4, m // 4, 128)
         low = lax.broadcasted_iota(jnp.int32, (m // 4, 128), 1) < 64
         for i in range(n // 8):
@@ -440,11 +426,10 @@
             turned = pltpu.roll(here, 64, 1)
             for k, value in ((0, jnp.where(low, here, turned)), (1, jnp.where(low, turned, here))):
                 f2[2 * i + k] = value
-                va[2 * i + k] = co[18] * value
-        now, later = va, vb
+        now, later = f2, va
         for k in range(COARSE - 2, -1, -1):
-            smooth(now, later, f2, co[18], co[19], 8 - k, n // 4 + 2 * k, 1)
-            now, later = later, now
+            smooth(now, later, f2, co[19], 8 - k, n // 4 + 2 * k, 1)
+            now, later = later, vb if later is va else va
 
         fine = choose(now[pl.ds(8, n // 4), pl.ds(0, m // 4)].reshape(n * m // 16, 128), back1[...])
         fine = fine.reshape(n // 4, m // 4, 128)
@@ -457,56 +442,107 @@
                 p = 4 + 2 * i + k
                 a1[p, pl.ds(0, m // 2)] = a1[p, pl.ds(0, m // 2)] + add
         finish(exchange(3, a1, a1, 4, n // 2, m // 2, m // 2 + 8, 3, 3))
-        smooth(a1, b1, f1, co[14], co[15], 2, n // 2 + 4, 1)
-        smooth(b1, a1, f1, co[14], co[15], 3, n // 2 + 2, 1)
-
-        fine = choose(a1[pl.ds(3, n // 2 + 2)].reshape((n // 2 + 2) * (m // 2 + 8), 128), back0[...])
-        xw[...] = fine.reshape(n // 2 + 2, m // 2 + 8, 256)
-
-        def widen(i, _):
-            for k in range(3):
-                g = 3 * i + k
-                for h in range(2):
-                    cut = pl.ds(128 * h, 128)
-                    near = xw[g, pl.ds(0, m // 2 + 2), cut]
-                    far = xw[g, pl.ds(m // 2 + 6, 2), cut]
-                    for e in range(2):
-                        w0[h, g, pl.ds(e, m // 2 + 2, stride=2)] = near
-                        w0[h, g, pl.ds(m + 4 + e, 2, stride=2)] = far
-                    add = w0[h, g]
-                    for e in range(2):
-                        a0[2 + 2 * g + e, :, cut] = a0[2 + 2 * g + e, :, cut] + add
-            return 0
-
-        lax.fori_loop(0, (n // 2 + 2) // 3, widen, 0)
-        smooth(a0, b0, f0, co[10], co[11], 3, n + 2, 2)
-        smooth(b0, a0, f0, co[10], co[11], 4, n, 2)
-
-    def turn(v, _):
-        @pl.when(v == VCYCLES)
-        def _():
-            second_right()
-
-        cycle()
+        smooth(a1, b1, f1, co[15], 2, n // 2 + 4, 1)
+        smooth(b1, a1, f1, co[15], 3, n // 2 + 2, 1)
+
+        for g in range(n // 2 + 2):
+            near = a1[3 + g, pl.ds(0, m // 2 + 2)]
+            far = a1[3 + g, pl.ds(m // 2 + 6, 2)]
+            for e in range(2):
+                w0[g, pl.ds(e, m // 2 + 2, stride=2)] = near
+                w0[g, pl.ds(m + 4 + e, 2, stride=2)] = far
+        for g in range(n // 2 + 2):
+            add = jnp.concatenate([w0[g], w0[g]], axis=1)
+            for e in range(2):
+                a0[2 + 2 * g + e] = a0[2 + 2 * g + e] + add
+        smooth(a0, b0, f0, co[11], 3, n + 2, 1)
+
+        smooth(b0, a0, f0, co[11], 4, 4, 1)
+        smooth(b0, a0, f0, co[11], n, 4, 1)
 
         @pl.when(v < SWEEPS * VCYCLES - 1)
         def _():
-            finish(exchange(0, a0, la, 4, n, m, m + 8, 4, 4))
-            land()
-
+            for copy in plane_faces():
+                copy.start()
+
+        for h in range(2):
+            smooth(b0, a0, f0, co[11], 8 + h * (n // 2 - 4), n // 2 - 4, 1)
+
+            @pl.when(v < SWEEPS * VCYCLES - 1)
+            def _():
+                for copy in row_faces(h):
+                    copy.start()
+
+    def plane_faces():
+        return exchange(
+            0, a0, la, 4, n, m, m + 8, 4, 4, [(a, b) for a in (-1, 1) for b in (-1, 0, 1)], start=False
+        )
+
+    def row_faces(h):
+        ps = pl.ds(4 + h * (n // 2), n // 2)
+        faces = []
+        for i, b in enumerate((-1, 1)):
+            qs, qd = span(b, m, 0, m + 4, 4)
+            faces.append(remote(a0.at[ps, qs], la.at[ps, qd], side_s.at[i, h], side_r.at[i, h], at(dz=b)))
+        return faces
+
+    def land_rows(h):
+        for copy in row_faces(h):
+            copy.wait_recv()
+        for k in range(n // 2):
+            p = 4 + h * (n // 2) + k
+            a0[p, pl.ds(m, 8)] = la[p, pl.ds(m, 8)]
+
+    def land_planes():
+        for copy in plane_faces():
+            copy.wait_recv()
+        for p in list(range(4)) + list(range(n + 4, n + 8)):
+            a0[p] = la[p]
+
+    def all_sent():
+        for copy in plane_faces() + row_faces(0) + row_faces(1):
+            copy.wait_send()
+
+    def turn(v, _):
+        @pl.when(lax.rem(v, VCYCLES) == 0)
+        def _():
+            @pl.when(v > 0)
+            def _():
+                land_rows(0)
+                land_rows(1)
+                land_planes()
+                second_right()
+                all_sent()
+
+            smooth(a0, b0, f0, co[11], 1, n + 6, 2)
+
+        @pl.when(lax.rem(v, VCYCLES) != 0)
+        def _():
+            land_rows(0)
+            smooth(a0, b0, f0, co[11], 5, n // 2 - 2, 1)
+            land_rows(1)
+            smooth(a0, b0, f0, co[11], n // 2 + 3, n // 2, 1)
+            land_planes()
+            smooth(a0, b0, f0, co[11], 1, 4, 1)
+            smooth(a0, b0, f0, co[11], n + 3, 4, 1)
+            all_sent()
+
+        cycle(v)
         return 0
 
     lax.fori_loop(0, SWEEPS * VCYCLES, turn, 0)
 
     def sent(d):
-        to = lax.rem(z + d, NZ)
-        src = a0.at[pl.ds(4 + 4 * to, 4), pl.ds(0, m), :]
+        src = ready.at[d]
         dst = out.at[:, pl.ds(pl.multiple_of(z * m, m), m), :]
         if d == 0:
             return pltpu.make_async_copy(src, dst, out_s.at[0])
         return remote(src, dst, out_s.at[d], out_r.at[d], at(dz=d))
 
     for d in (4, 3, 5, 2, 6, 1, 7, 0):
+        first = 4 + 4 * lax.rem(z + d, NZ)
+        block = a0[pl.ds(first, 4), pl.ds(0, m)].reshape(4 * m, 2 * half)
+        ready[d] = choose(block, joined[...]).reshape(4, m, 2 * half)
         sent(d).start()
     for d in (1, 7, 2, 6, 3, 5, 4):
         sent(d).wait_recv()
@@ -536,15 +572,14 @@
         out_specs=hbm,
         scratch_shapes=[
             pltpu.VMEM((2, n + 8, m + 8, cols), f32), full, full, full, full,
-            pltpu.VMEM((2, 2, 8, n // 8, m, cols), f32), chunks, chunks,
-            pltpu.VMEM((2, n // 2, m, cols // 2), f32), pltpu.VMEM((n // 2, m // 2, cols), f32),
-            pltpu.VMEM((2, n // 2 + 2, m + 8, cols // 2), f32), pltpu.VMEM((n // 2 + 2, m // 2 + 8, cols), f32),
+            pltpu.VMEM((2, 2, 8, n // 8, m, cols), f32), chunks, chunks, chunks,
+            pltpu.VMEM((n // 2, m, cols // 2), f32), pltpu.VMEM((n // 2 + 2, m + 8, cols // 2), f32),
             mid, mid, mid,
             pltpu.VMEM((n // 4, m // 2, cols // 2), f32), pltpu.VMEM((n // 4, m // 4, cols // 2), f32),
             pltpu.VMEM((n // 4, m // 2, cols // 2), f32),
             pltpu.VMEM((n // 8 + 8, m // 4 + 16, cols // 2), f32), low, low, low,
-            pick(cols, cols // 2), pick(cols // 2, cols // 2), pick(cols // 2, cols), pick(cols // 2, cols // 2),
-            dma((NZ,)), dma((NZ,)), dma((8, NZ)), dma((8, NZ)), dma((5, 8)), dma((5, 8)), dma((2, 8)), dma((2, 8)),
+            pick(cols, cols), pick(cols, cols), pick(cols // 2, cols // 2), pick(cols // 2, cols // 2),
+            dma((NZ,)), dma((NZ,)), dma((8, NZ)), dma((8, NZ)), dma((5, 8)), dma((5, 8)), dma((2, 8)), dma((2, 8)), dma((2, 2)), dma((2, 2)),
             dma((NZ,)), dma((NZ,)),
         ],
         compiler_params=pltpu.CompilerParams(collective_id=0, has_side_effects=True, vmem_limit_bytes=60 * 2**20),

time: 185 us -> 173 us (0.935)
  Pallas kernels: 182 us -> 170 us
    pallas_call x1, Pallas kernels: 182 us -> 170 us  [per_device(): pl.pallas_call(kernel, out_shape=jax.ShapeDtypeStruct((thick, rows, cols)...]
where the time goes in v2:
time: 173 us
  Pallas kernels  170 us (98%)
  local copies, waits for them, and re-layouts  2.29 us (1%)
    pallas_call x1, Pallas kernels, per_device(): pl.pallas_call(kernel, out_shape=jax.ShapeDtypeStruct((thick, rows, cols)...  170 us

profile of v2, /device:TPU:2, one launch (start us, length us, event | category | flops | bytes accessed | tf_op | source)
XLA Modules:
  0.0 172.7 jit_solution(8699749518512178128)
XLA Ops:
  0.0 170.4 %shard_map.37 = f32[4,256,256]{2,1,0:T(8,128)} custom-call(f32[192]{0:T(256)} %constant.2.clone.table, f32[4,256,256]{2,1,0:T(8,128)} %initial.1, f32[4,256,256]{2,1,0:T(8,128)} %kappa.1), custom_call_target="tpu_custom_call" | custom-call | tf_op jit(solution)/shard_map/pallas_call | solution.py:568
  170.4 2.3 %copy.5 = f32[1,4,256,256]{3,2,1,0:T(8,128)} copy(f32[1,4,256,256]{3,2,1,0:T(8,128)} %bitcast.1) | data formatting | bytes 2097152

commit v3 on v2

--- a/solution.py
+++ b/solution.py
@@ -20,7 +20,7 @@
 NY = 4
 NZ = 8
 NX = 4
-DIRS = [(a, b) for a in (-1, 0, 1) for b in (-1, 0, 1) if (a, b) != (0, 0)]
+DIRS = [(-1, -1), (-1, 1), (1, -1), (1, 1), (-1, 0), (1, 0), (0, -1), (0, 1)]
 
 
 def radau_gap(count, where):
@@ -142,17 +142,16 @@
 
 
 def kernel(
-    table, initial, kappa, out,
-    uk, a0, b0, f0, la, fg, sums, come, ready, rs, w0,
+    numbers, initial, kappa, out,
+    table, uk, a0, b0, f0, la, fg, sums, come, ready, rs, w0,
     a1, b1, f1, rs1, st1, w1, pk, f2, va, vb, apart, joined, pick1, back1,
-    in_s, in_r, xi, xq, halo_s, halo_r, rows_s, rows_r, side_s, side_r, out_s, out_r,
+    in_s, in_r, xi, xq, halo_s, halo_r, rows_s, rows_r, side_s, side_r, out_s, out_r, table_s,
 ):
     node = lax.axis_index("node")
     space = lax.axis_index("space")
     x, core = node // 2, lax.rem(node, 2)
     y, z = space // NZ, lax.rem(space, NZ)
     n, m = NZ * 4, a0.shape[1] - 8
-    co = [table[node * ROW + i] for i in range(20)]
 
     def at(dx=0, dc=0, dy=0, dz=0):
         nx = lax.rem(x + dx + NX, NX)
@@ -164,6 +163,8 @@
     peers = [at(dz=d) for d in range(1, NZ)]
     peers += [at(dy=a, dz=b) for a in (-1, 1) for b in (-1, 0, 1)]
     peers += [at(dx=1), at(dx=-1), at(dc=1)]
+    fetch = pltpu.make_async_copy(numbers, table, table_s.at[0])
+    fetch.start()
     barrier = pltpu.get_barrier_semaphore()
     for peer in peers:
         pl.semaphore_signal(barrier, inc=1, device_id=peer, device_id_type=MESH)
@@ -239,8 +240,10 @@
 
     order = (0, 1, 7, 2, 6, 3, 5, 4)
     left, right = lax.rem(x + NX - 1, NX), lax.rem(x + 1, NX)
-    own, passed, cores = {}, {}, {}
-    for q in order:
+    mine = uk.at[core]
+    own, passed, cores, faces = {}, {}, {}, []
+
+    def arrived(q):
         if q == 0:
             fetched(initial, q).wait()
         else:
@@ -253,7 +256,8 @@
         ]
         for copy in own[q]:
             copy.start()
-    for q in order:
+
+    def pass_on(q):
         own[q][0].wait_recv()
         if q % 2 == 0:
             passed[q] = remote(in_piece(left, q), in_piece(left, q), xi.at[4, q], xi.at[5, q], at(dx=1))
@@ -262,23 +266,52 @@
         if q % 2 == 1:
             passed[q] = remote(in_piece(right, q), in_piece(right, q), xi.at[4, q], xi.at[5, q], at(dx=-1))
             passed[q].start()
-    for q in order:
+
+    def first_faces(a, start):
+        return exchange(0, mine, mine, 4, n, m, m + 8, 4, 4, [(a, b) for b in (-1, 0, 1)], start)
+
+    def complete(q):
         passed[q].wait_recv()
+        come_z = lax.rem(z + NZ - q, NZ)
+        ps = pl.ds(4 + 4 * come_z, 4)
+        for i, b in enumerate((-1, 1)):
+            qs, qd = span(b, m, 0, m + 4, 4)
+            faces.append(remote(mine.at[ps, qs], mine.at[ps, qd], rows_s.at[i, q], rows_r.at[i, q], at(dz=b)))
+            faces[-1].start()
+        for a, end in ((-1, 0), (1, NZ - 1)):
+
+            @pl.when(come_z == end)
+            def _():
+                first_faces(a, True)
+
         cores[q] = remote(in_both(q), in_both(q), xi.at[6, q], xi.at[7, q], at(dc=1))
         cores[q].start()
-    mine = uk.at[core]
-    finish(exchange(0, mine, mine, 4, n, m, m + 8, 4, 4))
+
+    for i in range(NZ + 4):
+        if i < NZ:
+            arrived(order[i])
+        if 2 <= i < NZ + 2:
+            pass_on(order[i - 2])
+        if 4 <= i:
+            complete(order[i - 4])
+    for q in order:
+        cores[q].wait_recv()
+
+    def fill(i, _):
+        for k in range(4):
+            a0[4 + i * 4 + k, pl.ds(0, m)] = uk[0, 4 + i * 4 + k, pl.ds(0, m)]
+        return 0
+
+    lax.fori_loop(0, n // 4, fill, 0)
+    finish(faces + first_faces(-1, False) + first_faces(1, False))
     edges = [
         uk.at[core, pl.ds(0, 4)],
         uk.at[core, pl.ds(n + 4, 4)],
         uk.at[core, pl.ds(4, n), pl.ds(m, 8)],
     ]
-    given = [remote(e, e, rows_s.at[0, i], rows_r.at[0, i], at(dc=1)) for i, e in enumerate(edges)]
+    given = [remote(e, e, side_s.at[i // 2, i % 2], side_r.at[i // 2, i % 2], at(dc=1)) for i, e in enumerate(edges)]
     for copy in given:
         copy.start()
-    for q in order:
-        cores[q].wait_recv()
-    finish(given)
     for q in order:
         own[q][0].wait_send()
         own[q][1].wait_send()
@@ -286,13 +319,19 @@
         cores[q].wait_send()
     for d in range(1, NZ):
         fetched(initial, d).wait_send()
-
-    def fill(i, _):
-        for k in range(4):
-            a0[i * 4 + k] = uk[0, i * 4 + k]
+    finish(given)
+    for p in list(range(4)) + list(range(n + 4, n + 8)):
+        a0[p] = uk[0, p]
+
+    def fill_rows(i, _):
+        for k in range(8):
+            a0[4 + i * 8 + k, pl.ds(m, 8)] = uk[0, 4 + i * 8 + k, pl.ds(m, 8)]
         return 0
 
-    lax.fori_loop(0, (n + 8) // 4, fill, 0)
+    lax.fori_loop(0, n // 8, fill_rows, 0)
+
+    fetch.wait()
+    co = [table[node * ROW + i] for i in range(20)]
 
     shift, rowsum = co[8], co[9]
 
@@ -567,10 +606,11 @@
     hbm = pl.BlockSpec(memory_space=pl.ANY)
     result = pl.pallas_call(
         kernel,
-        out_shape=jax.ShapeDtypeStruct((thick, rows, cols), f32),
-        in_specs=[pl.BlockSpec(memory_space=pltpu.SMEM), hbm, hbm],
-        out_specs=hbm,
+        out_shape=pltpu.VMEM((thick, rows, cols), f32),
+        in_specs=[hbm, hbm, hbm],
+        out_specs=pl.BlockSpec(memory_space=pltpu.VMEM),
         scratch_shapes=[
+            pltpu.SMEM((count * ROW,), f32),
             pltpu.VMEM((2, n + 8, m + 8, cols), f32), full, full, full, full,
             pltpu.VMEM((2, 2, 8, n // 8, m, cols), f32), chunks, chunks, chunks,
             pltpu.VMEM((n // 2, m, cols // 2), f32), pltpu.VMEM((n // 2 + 2, m + 8, cols // 2), f32),
@@ -580,7 +620,7 @@
             pltpu.VMEM((n // 8 + 8, m // 4 + 16, cols // 2), f32), low, low, low,
             pick(cols, cols), pick(cols, cols), pick(cols // 2, cols // 2), pick(cols // 2, cols // 2),
             dma((NZ,)), dma((NZ,)), dma((8, NZ)), dma((8, NZ)), dma((5, 8)), dma((5, 8)), dma((2, 8)), dma((2, 8)), dma((2, 2)), dma((2, 2)),
-            dma((NZ,)), dma((NZ,)),
+            dma((NZ,)), dma((NZ,)), dma((1,)),
         ],
         compiler_params=pltpu.CompilerParams(collective_id=0, has_side_effects=True, vmem_limit_bytes=60 * 2**20),
     )(jnp.asarray(coefficients(count)), initial, kappa)

time: 173 us -> 169 us (0.977)
  Pallas kernels: 170 us -> 168 us
    pallas_call x1, Pallas kernels: 170 us -> 168 us  [per_device(): pl.pallas_call(kernel, out_shape=pltpu.VMEM((thick, rows, cols), f32), in...]
where the time goes in v3:
time: 169 us
  Pallas kernels  168 us (99%)
    pallas_call x1, Pallas kernels, per_device(): pl.pallas_call(kernel, out_shape=pltpu.VMEM((thick, rows, cols), f32), in...  168 us

profile of v3, /device:TPU:2, one launch (start us, length us, event | category | flops | bytes accessed | tf_op | source)
XLA Modules:
  0.0 168.5 jit_solution(17748095932612938786)
XLA Ops:
  0.0 167.6 %shard_map.37 = f32[4,256,256]{2,1,0:T(8,128)S(1)} custom-call(f32[192]{0:T(256)} %constant.2.clone.numbers, f32[4,256,256]{2,1,0:T(8,128)} %initial.1, f32[4,256,256]{2,1,0:T(8,128)} %kappa.1), custom_call_target="tpu_custom_call" | custom-call | tf_op jit(solution)/shard_map/pallas_call | solution.py:607
  167.6 1.0 copy.5

commit v4 on v3

--- a/solution.py
+++ b/solution.py
@@ -21,6 +21,7 @@
 NZ = 8
 NX = 4
 DIRS = [(-1, -1), (-1, 1), (1, -1), (1, 1), (-1, 0), (1, 0), (0, -1), (0, 1)]
+OTHERS, ROWS = slice(0, 6), slice(6, 8)
 
 
 def radau_gap(count, where):
@@ -303,14 +304,36 @@
         return 0
 
     lax.fori_loop(0, n // 4, fill, 0)
-    finish(faces + first_faces(-1, False) + first_faces(1, False))
-    edges = [
-        uk.at[core, pl.ds(0, 4)],
-        uk.at[core, pl.ds(n + 4, 4)],
-        uk.at[core, pl.ds(4, n), pl.ds(m, 8)],
-    ]
-    given = [remote(e, e, side_s.at[i // 2, i % 2], side_r.at[i // 2, i % 2], at(dc=1)) for i, e in enumerate(edges)]
-    for copy in given:
+    def give(i, ref):
+        return remote(ref, ref, side_s.at[i // 2, i % 2], side_r.at[i // 2, i % 2], at(dc=1))
+
+    fetch.wait()
+    co = [table[node * ROW + i] for i in range(20)]
+    shift, rowsum = co[8], co[9]
+
+    def first_right(p, here, total):
+        lap = total - 6.0 * here
+        force = DIFFUSE * lap + REACT * uk[1, p] * (here - here * here * here)
+        f0[p] = co[10] * (here + (rowsum * force - shift * lap))
+
+    for copy in faces:
+        copy.wait_recv()
+    given = [give(0, mine.at[pl.ds(4, n), pl.ds(m, 8)])]
+    given[0].start()
+    given[0].wait_recv()
+
+    def fill_rows(i, _):
+        for k in range(8):
+            a0[4 + i * 8 + k, pl.ds(m, 8)] = uk[0, 4 + i * 8 + k, pl.ds(m, 8)]
+        return 0
+
+    lax.fori_loop(0, n // 8, fill_rows, 0)
+    sweep_planes(a0, 5, n - 2, 2, first_right)
+    ends = first_faces(-1, False) + first_faces(1, False)
+    for copy in ends:
+        copy.wait_recv()
+    given += [give(1, mine.at[pl.ds(0, 4)]), give(2, mine.at[pl.ds(n + 4, 4)])]
+    for copy in given[1:]:
         copy.start()
     for q in order:
         own[q][0].wait_send()
@@ -319,28 +342,16 @@
         cores[q].wait_send()
     for d in range(1, NZ):
         fetched(initial, d).wait_send()
-    finish(given)
+    for copy in faces + ends:
+        copy.wait_send()
+    for copy in given[1:]:
+        copy.wait_recv()
+    for copy in given:
+        copy.wait_send()
     for p in list(range(4)) + list(range(n + 4, n + 8)):
         a0[p] = uk[0, p]
-
-    def fill_rows(i, _):
-        for k in range(8):
-            a0[4 + i * 8 + k, pl.ds(m, 8)] = uk[0, 4 + i * 8 + k, pl.ds(m, 8)]
-        return 0
-
-    lax.fori_loop(0, n // 8, fill_rows, 0)
-
-    fetch.wait()
-    co = [table[node * ROW + i] for i in range(20)]
-
-    shift, rowsum = co[8], co[9]
-
-    def first_right(p, here, total):
-        lap = total - 6.0 * here
-        force = DIFFUSE * lap + REACT * uk[1, p] * (here - here * here * here)
-        f0[p] = co[10] * (here + (rowsum * force - shift * lap))
-
-    sweep_planes(a0, 1, n + 6, 2, first_right)
+    sweep_planes(a0, 1, 4, 1, first_right)
+    sweep_planes(a0, n + 3, 4, 1, first_right)
 
     def second_right():
         def toward(q):
@@ -438,9 +449,17 @@
             f1[4 + i, pl.ds(0, m // 2)] = mean * (
                 rs[i, pl.ds(0, m // 2, stride=2)] + rs[i, pl.ds(1, m // 2, stride=2)]
             )
-        finish(exchange(1, f1, f1, 4, n // 2, m // 2, m // 2 + 8, 2, 2))
-
-        smooth(f1, a1, f1, co[15], 3, n // 2 + 2, 1)
+        copies = exchange(1, f1, f1, 4, n // 2, m // 2, m // 2 + 8, 2, 2)
+        for copy in copies[ROWS]:
+            copy.wait_recv()
+
+        smooth(f1, a1, f1, co[15], 5, n // 2 - 2, 1)
+        for copy in copies[OTHERS]:
+            copy.wait_recv()
+        smooth(f1, a1, f1, co[15], 3, 2, 1)
+        smooth(f1, a1, f1, co[15], n // 2 + 3, 2, 1)
+        for copy in copies:
+            copy.wait_send()
 
         def rest1(p, here, total):
             held.append((f1[p] - OMEGA * here + co[15] * total)[: m // 2])
@@ -480,8 +499,16 @@
             for k in range(2):
                 p = 4 + 2 * i + k
                 a1[p, pl.ds(0, m // 2)] = a1[p, pl.ds(0, m // 2)] + add
-        finish(exchange(3, a1, a1, 4, n // 2, m // 2, m // 2 + 8, 3, 3))
-        smooth(a1, b1, f1, co[15], 2, n // 2 + 4, 1)
+        copies = exchange(3, a1, a1, 4, n // 2, m // 2, m // 2 + 8, 3, 3)
+        for copy in copies[ROWS]:
+            copy.wait_recv()
+        smooth(a1, b1, f1, co[15], 5, n // 2 - 2, 1)
+        for copy in copies[OTHERS]:
+            copy.wait_recv()
+        smooth(a1, b1, f1, co[15], 2, 3, 1)
+        smooth(a1, b1, f1, co[15], n // 2 + 3, 3, 1)
+        for copy in copies:
+            copy.wait_send()
         smooth(b1, a1, f1, co[15], 3, n // 2 + 2, 1)
 
         for g in range(n // 2 + 2):

time: 169 us -> 170 us (level)
  no operation moved by 1% of the time
where the time goes in v4:
time: 170 us; the launch traced here: 169 us
  Pallas kernels  168 us (99%)
    pallas_call x1, Pallas kernels, per_device(): pl.pallas_call(kernel, out_shape=pltpu.VMEM((thick, rows, cols), f32), in...  168 us

profile of v4, /device:TPU:2, one launch (start us, length us, event | category | flops | bytes accessed | tf_op | source)
XLA Modules:
  0.0 168.7 jit_solution(13487681803592536854)
XLA Ops:
  0.0 167.8 %shard_map.37 = f32[4,256,256]{2,1,0:T(8,128)S(1)} custom-call(f32[192]{0:T(256)} %constant.2.clone.numbers, f32[4,256,256]{2,1,0:T(8,128)} %initial.1, f32[4,256,256]{2,1,0:T(8,128)} %kappa.1), custom_call_target="tpu_custom_call" | custom-call | tf_op jit(solution)/shard_map/pallas_call | solution.py:634
  167.8 1.0 copy.5
